TPU v7x, 32 devices: a 4x4x1 block of a 4x4x8 slice. The times are simulated.
32 devices in a mesh: dp: 1 (over z), sw: 4 (over y), sh: 8 (over x, core).
Axes of the slice: x: 4, y: 4, z: 1, core: 2. Of those that a mesh axis runs over, the one named last changes fastest.
The devices are a block of a 4x4x8 slice.
Arguments:
- features: bfloat16 [1, 768, 3, 64, 32], P('dp', None, None, 'sh', 'sw')
- latent: bfloat16 [1, 12, 3, 64, 32], P('dp', None, None, 'sh', 'sw')
- gn_gain: float32 [2, 2, 768], replicated
- gn_bias: float32 [2, 2, 768], replicated
- zy_weight: bfloat16 [2, 2, 12, 768], replicated
- zy_bias: float32 [2, 2, 768], replicated
- zb_weight: bfloat16 [2, 2, 12, 768], replicated
- zb_bias: float32 [2, 2, 768], replicated
- conv_weight: bfloat16 [2, 2, 768, 768, 3, 3, 3], replicated
- conv_bias: float32 [2, 2, 768], replicated
- up_weight: bfloat16 [768, 768, 3, 3], replicated
- up_bias: float32 [768], replicated
Outputs:
- output: bfloat16 [1, 768, 3, 128, 64], P('dp', None, None, 'sh', 'sw')
All inputs are finite; a program needn't handle non-finite values.
Results may differ from a plain program's by a relative error of at most 0.0125931.
Values are sent between devices in bfloat16 or wider.
A program may use at most 768 MiB of HBM per device.

v0:
```python
import jax
import jax.numpy as jnp
from jax import lax
from jax.sharding import PartitionSpec as P

NUM_GROUPS = 32
GN_EPSILON = 1e-6
CONV_DIMS = ("NCDHW", "OIDHW", "NCDHW")


def solution(mesh):
    n_sh = mesh.shape["sh"]
    n_sw = mesh.shape["sw"]

    def per_channel(values):
        return values[None, :, None, None, None]

    def edge_exchange(values, axis_name, n_dev, dim):
        n_len = values.shape[dim]
        tail = lax.slice_in_dim(values, n_len - 1, n_len, axis=dim)
        head = lax.slice_in_dim(values, 0, 1, axis=dim)
        if n_dev == 1:
            from_prev = jnp.zeros_like(tail)
            from_next = jnp.zeros_like(head)
        else:
            from_prev = lax.ppermute(tail, axis_name, [(i, i + 1) for i in range(n_dev - 1)])
            from_next = lax.ppermute(head, axis_name, [(i + 1, i) for i in range(n_dev - 1)])
        return jnp.concatenate([from_prev, values, from_next], axis=dim)

    def with_border(values):
        return edge_exchange(edge_exchange(values, "sh", n_sh, 3), "sw", n_sw, 4)

    def group_norm(values, gain, shift):
        n_batch, n_chan, n_frame, n_row, n_col = values.shape
        grouped = values.astype(jnp.float32).reshape(n_batch, NUM_GROUPS, n_chan // NUM_GROUPS, n_frame, n_row, n_col)
        local_stats = jnp.stack([jnp.sum(grouped, axis=(2, 3, 4, 5)), jnp.sum(jnp.square(grouped), axis=(2, 3, 4, 5))])
        total_stats = lax.psum(local_stats, ("sh", "sw"))
        count = (n_chan // NUM_GROUPS) * n_frame * n_row * n_col * n_sh * n_sw
        group_mean = total_stats[0] / count
        group_var = jnp.maximum(total_stats[1] / count - jnp.square(group_mean), 0.0)
        inv_std = lax.rsqrt(group_var + GN_EPSILON)
        normed = (grouped - group_mean[:, :, None, None, None, None]) * inv_std[:, :, None, None, None, None]
        return normed.reshape(values.shape) * per_channel(gain) + per_channel(shift)

    def latent_map(latent, weight, bias):
        return jnp.einsum("nzthw,zc->ncthw", latent, weight, preferred_element_type=jnp.float32) + per_channel(bias)

    def causal_conv(bordered, weight, bias):
        first_frame = bordered[:, :, :1]
        padded = jnp.concatenate([first_frame, first_frame, bordered], axis=2)
        conv_out = lax.conv_general_dilated(padded, weight, (1, 1, 1), "VALID", dimension_numbers=CONV_DIMS, preferred_element_type=jnp.float32)
        return (conv_out + per_channel(bias)).astype(jnp.bfloat16)

    def upsample_conv(bordered, weight, bias):
        upsampled = jnp.repeat(jnp.repeat(bordered, 2, axis=3), 2, axis=4)
        n_row = upsampled.shape[3]
        n_col = upsampled.shape[4]
        cropped = upsampled[:, :, :, 1:n_row - 1, 1:n_col - 1]
        conv_out = lax.conv_general_dilated(cropped, weight[:, :, None], (1, 1, 1), "VALID", dimension_numbers=CONV_DIMS, preferred_element_type=jnp.float32)
        return (conv_out + per_channel(bias)).astype(jnp.bfloat16)

    def local_step(features, latent, gn_gain, gn_bias, zy_weight, zy_bias, zb_weight, zb_bias, conv_weight, conv_bias, up_weight, up_bias):
        hidden = features
        for block in range(gn_gain.shape[0]):
            branch = hidden
            for slot in range(2):
                normed = group_norm(branch, gn_gain[block, slot], gn_bias[block, slot])
                mixed = normed * latent_map(latent, zy_weight[block, slot], zy_bias[block, slot]) + latent_map(latent, zb_weight[block, slot], zb_bias[block, slot])
                activated = jax.nn.silu(mixed).astype(jnp.bfloat16)
                branch = causal_conv(with_border(activated), conv_weight[block, slot], conv_bias[block, slot])
            hidden = (hidden.astype(jnp.float32) + branch.astype(jnp.float32)).astype(jnp.bfloat16)
        return upsample_conv(with_border(hidden), up_weight, up_bias)

    data_spec = P("dp", None, None, "sh", "sw")
    return jax.shard_map(local_step, mesh=mesh, in_specs=(data_spec, data_spec) + (P(),) * 10, out_specs=data_spec, check_vma=False)
```

profile of v0, /device:TPU:97, one launch (start us, length us, event | category | flops | bytes accessed | tf_op | source)
XLA Modules:
  0.0 443.7 jit_solution(13242790254548362293)
XLA Ops:
  1.5 49.8 %psum.28 = f32[2,1,32]{2,1,0:T(1,128)S(1)} all-reduce(f32[2,1,32]{2,1,0:T(1,128)S(1)} %pad_maximum_fusion.31), channel_id=1, replica_groups=mesh['dp'=1,'sw'=4,'sh'=8] {'sh','sw'}, use_global_device_ids=true, to_apply=%region_4.5 | all-reduce | flops 64 | bytes 512 | tf_op jit(solution)/shard_map/psum | solution.py:37
  59.8 2.4 collective-permute-start.1
  62.6 2.4 collective-permute-done.1
  65.2 2.4 collective-permute-start.2
  70.0 2.9 collective-permute-done.3
  73.5 34.7 %fusion.6 = f32[1,768,3,8,8]{1,0,4,3,2:T(1,128)S(1)} fusion(bf16[2,2,768,768,3,3,3]{3,2,6,5,4,1,0:T(8,128)(2,1)} %param.20, bf16[1,768,5,10,10]{1,4,3,2,0:T(8,128)(2,1)S(1)} %maximum_maximum_fusion), kind=kOutput, calls=%fused_computation.6 | convolution fusion | flops 6115295232 | bytes 33208320 | tf_op jit(solution)/shard_map/conv_general_dilated | solution.py:51
  108.8 45.2 %psum.29 = f32[2,1,32]{2,1,0:T(1,128)S(1)} all-reduce(f32[2,1,32]{2,1,0:T(1,128)S(1)} %pad_maximum_fusion.32), channel_id=1, replica_groups=mesh['dp'=1,'sw'=4,'sh'=8] {'sh','sw'}, use_global_device_ids=true, to_apply=%region_9.10 | all-reduce | flops 64 | bytes 512 | tf_op jit(solution)/shard_map/psum | solution.py:37
  154.6 2.1 collective-permute-start.4
  156.7 2.3 collective-permute-start.5
  159.2 2.8 collective-permute-done.5
  162.1 2.3 collective-permute-start.6
  166.1 3.6 collective-permute-done.7
  170.4 34.5 %fusion.4 = f32[1,768,3,8,8]{1,0,4,3,2:T(1,128)S(1)} fusion(bf16[2,2,768,768,3,3,3]{3,2,6,5,4,1,0:T(8,128)(2,1)} %param.20, bf16[1,768,5,10,10]{1,4,3,2,0:T(8,128)(2,1)S(1)} %maximum_maximum_fusion.1), kind=kOutput, calls=%fused_computation.4 | convolution fusion | flops 6115295232 | bytes 33208320 | tf_op jit(solution)/shard_map/conv_general_dilated | solution.py:51
  205.6 45.5 %psum.30 = f32[2,1,32]{2,1,0:T(1,128)S(1)} all-reduce(f32[2,1,32]{2,1,0:T(1,128)S(1)} %pad_maximum_fusion.33), channel_id=1, replica_groups=mesh['dp'=1,'sw'=4,'sh'=8] {'sh','sw'}, use_global_device_ids=true, to_apply=%region_14.15 | all-reduce | flops 64 | bytes 512 | tf_op jit(solution)/shard_map/psum | solution.py:37
  253.8 2.3 collective-permute-start.9
  256.4 2.8 collective-permute-done.9
  259.3 2.3 collective-permute-start.10
  263.1 3.8 collective-permute-done.11
  267.5 34.8 %fusion.2 = f32[1,768,3,8,8]{1,0,4,3,2:T(1,128)S(1)} fusion(bf16[2,2,768,768,3,3,3]{3,2,6,5,4,1,0:T(8,128)(2,1)} %param.20, bf16[1,768,5,10,10]{1,4,3,2,0:T(8,128)(2,1)S(1)} %maximum_maximum_fusion.2), kind=kOutput, calls=%fused_computation.2 | convolution fusion | flops 6115295232 | bytes 33208320 | tf_op jit(solution)/shard_map/conv_general_dilated | solution.py:51
  302.9 45.2 %psum.31 = f32[2,1,32]{2,1,0:T(1,128)S(1)} all-reduce(f32[2,1,32]{2,1,0:T(1,128)S(1)} %pad_maximum_fusion.34), channel_id=1, replica_groups=mesh['dp'=1,'sw'=4,'sh'=8] {'sh','sw'}, use_global_device_ids=true, to_apply=%region_19.20 | all-reduce | flops 64 | bytes 512 | tf_op jit(solution)/shard_map/psum | solution.py:37
  350.9 2.3 collective-permute-start.13
  353.3 3.0 collective-permute-done.13
  356.4 2.3 collective-permute-start.14
  360.2 3.8 collective-permute-done.15
  364.6 34.5 %fusion = f32[1,768,3,8,8]{1,0,4,3,2:T(1,128)S(1)} fusion(bf16[2,2,768,768,3,3,3]{3,2,6,5,4,1,0:T(8,128)(2,1)} %param.20, bf16[1,768,5,10,10]{1,4,3,2,0:T(8,128)(2,1)S(1)} %maximum_maximum_fusion.3), kind=kOutput, calls=%fused_computation | convolution fusion | flops 6115295232 | bytes 33208320 | tf_op jit(solution)/shard_map/conv_general_dilated | solution.py:51
  399.3 4.2 collective-permute-start.16
  405.4 3.3 collective-permute-done.17
  408.9 2.7 collective-permute-start.18
  413.2 3.8 collective-permute-done.19
  417.5 2.3 broadcast_in_dim.24
  419.8 4.2 reshape.402
  426.5 15.1 %add_convert_fusion = bf16[3,16,8,3,768]{4,2,3,1,0:T(8,128)(2,1)S(1)} fusion(bf16[768,768,3,3]{1,0,3,2:T(8,128)(2,1)} %param.22, bf16[768,3,20,1,7,2]{0,4,5,2,1,3:T(8,128)(2,1)S(1)} %slice.278, bf16[768,3,20,1,8,3]{0,4,5,2,1,3:T(8,128)(2,1)S(1)} %copy.50, f32[768]{0:T(1024)S(1)} %copy-done.21, pred[8,3]{0,1:T(4,128)(4,1)S(1)} %copy-done.22), kind=kOutput, calls=%fused_computation.21 | convolution fusion | flops 12244303872 | bytes 15891480 | tf_op jit(solution)/shard_map/conv_general_dilated | solution.py:59
  (158 shorter events, 36.9 us)
Async XLA Ops:
  0.0 57.5 %copy-start.1 = (bf16[1,768,3,8,8]{1,4,3,2,0:T(8,128)(2,1)S(1)}, bf16[1,768,3,8,8]{1,4,3,2,0:T(8,128)(2,1)}, u32[]{:S(2)}) copy-start(bf16[1,768,3,8,8]{1,4,3,2,0:T(8,128)(2,1)} %param.12) | copy-start | bytes 884740
  0.0 56.8 %copy-start.18 = (f32[2,2,768]{2,1,0:T(2,128)S(1)}, f32[2,2,768]{2,1,0:T(2,128)}, u32[]{:S(2)}) copy-start(f32[2,2,768]{2,1,0:T(2,128)} %param.19) | copy-start | bytes 36868
  57.8 4.8 %collective-permute-start = (bf16[1,768,3,1,8]{1,4,3,2,0:T(8,128)(2,1)S(1)}, bf16[1,768,3,1,8]{1,4,3,2,0:T(8,128)(2,1)S(1)}, u32[]{:S(2)}, u32[]{:S(2)}) collective-permute-start(bf16[1,768,3,1,8]{1,4,3,2,0:T(8,128)(2,1)S(1)} %get-tuple-element.54), channel_id=1, source_target_pairs={{0,1},{1,2},{2,3},{3,4},{4,5},{5,6},{6,7},{8,9},{9,10},{10,11},{11... | collective-permute-start | bytes 110600 | tf_op jit(solution)/shard_map/ppermute | solution.py:26
  59.8 5.3 %collective-permute-start.1 = (bf16[1,768,3,1,8]{1,4,3,2,0:T(8,128)(2,1)S(1)}, bf16[1,768,3,1,8]{1,4,3,2,0:T(8,128)(2,1)S(1)}, u32[]{:S(2)}, u32[]{:S(2)}) collective-permute-start(bf16[1,768,3,1,8]{1,4,3,2,0:T(8,128)(2,1)S(1)} %get-tuple-element.55), channel_id=1, source_target_pairs={{1,0},{2,1},{3,2},{4,3},{5,4},{6,5},{7,6},{9,8},{10,9},{11,10},{12... | collective-permute-start | bytes 110600 | tf_op jit(solution)/shard_map/ppermute | solution.py:27
  65.2 4.9 %collective-permute-start.2 = (bf16[1,768,3,10,1]{1,4,3,2,0:T(2,128)(2,1)S(1)}, bf16[1,768,3,10,1]{1,4,3,2,0:T(2,128)(2,1)S(1)}, u32[]{:S(2)}, u32[]{:S(2)}) collective-permute-start(bf16[1,768,3,10,1]{1,4,3,2,0:T(2,128)(2,1)S(1)} %get-tuple-element.44), channel_id=1, source_target_pairs={{0,8},{8,16},{16,24},{1,9},{9,17},{17,25},{2,10},{10,18},{18,26},{... | collective-permute-start | bytes 138248 | tf_op jit(solution)/shard_map/ppermute | solution.py:26
  67.6 5.3 %collective-permute-start.3 = (bf16[1,768,3,10,1]{1,4,3,2,0:T(2,128)(2,1)S(1)}, bf16[1,768,3,10,1]{1,4,3,2,0:T(2,128)(2,1)S(1)}, u32[]{:S(2)}, u32[]{:S(2)}) collective-permute-start(bf16[1,768,3,10,1]{1,4,3,2,0:T(2,128)(2,1)S(1)} %get-tuple-element.45), channel_id=1, source_target_pairs={{8,0},{16,8},{24,16},{9,1},{17,9},{25,17},{10,2},{18,10},{26,18},{... | collective-permute-start | bytes 138248 | tf_op jit(solution)/shard_map/ppermute | solution.py:27
  154.6 4.6 %collective-permute-start.4 = (bf16[1,768,3,1,8]{1,4,3,2,0:T(8,128)(2,1)S(1)}, bf16[1,768,3,1,8]{1,4,3,2,0:T(8,128)(2,1)S(1)}, u32[]{:S(2)}, u32[]{:S(2)}) collective-permute-start(bf16[1,768,3,1,8]{1,4,3,2,0:T(8,128)(2,1)S(1)} %get-tuple-element.52), channel_id=1, source_target_pairs={{0,1},{1,2},{2,3},{3,4},{4,5},{5,6},{6,7},{8,9},{9,10},{10,11},{11... | collective-permute-start | bytes 110600 | tf_op jit(solution)/shard_map/ppermute | solution.py:26
  156.7 5.3 %collective-permute-start.5 = (bf16[1,768,3,1,8]{1,4,3,2,0:T(8,128)(2,1)S(1)}, bf16[1,768,3,1,8]{1,4,3,2,0:T(8,128)(2,1)S(1)}, u32[]{:S(2)}, u32[]{:S(2)}) collective-permute-start(bf16[1,768,3,1,8]{1,4,3,2,0:T(8,128)(2,1)S(1)} %get-tuple-element.53), channel_id=1, source_target_pairs={{1,0},{2,1},{3,2},{4,3},{5,4},{6,5},{7,6},{9,8},{10,9},{11,10},{12... | collective-permute-start | bytes 110600 | tf_op jit(solution)/shard_map/ppermute | solution.py:27
  162.1 4.0 collective-permute-start.6
  164.4 5.3 %collective-permute-start.7 = (bf16[1,768,3,10,1]{1,4,3,2,0:T(2,128)(2,1)S(1)}, bf16[1,768,3,10,1]{1,4,3,2,0:T(2,128)(2,1)S(1)}, u32[]{:S(2)}, u32[]{:S(2)}) collective-permute-start(bf16[1,768,3,10,1]{1,4,3,2,0:T(2,128)(2,1)S(1)} %get-tuple-element.43), channel_id=1, source_target_pairs={{8,0},{16,8},{24,16},{9,1},{17,9},{25,17},{10,2},{18,10},{26,18},{... | collective-permute-start | bytes 138248 | tf_op jit(solution)/shard_map/ppermute | solution.py:27
  170.3 81.0 %copy-start.11 = (f32[768]{0:T(1024)S(1)}, f32[768]{0:T(1024)}, u32[]{:S(2)}) copy-start(f32[768]{0:T(1024)} %get-tuple-element.21) | copy-start | bytes 9220
  170.4 81.0 %copy-start.12 = (f32[768]{0:T(1024)S(1)}, f32[768]{0:T(1024)}, u32[]{:S(2)}) copy-start(f32[768]{0:T(1024)} %get-tuple-element.71) | copy-start | bytes 9220
  170.4 81.0 %copy-start.13 = (f32[768]{0:T(1024)S(1)}, f32[768]{0:T(1024)}, u32[]{:S(2)}) copy-start(f32[768]{0:T(1024)} %get-tuple-element.29) | copy-start | bytes 9220
  170.4 81.0 %copy-start.14 = (f32[768]{0:T(1024)S(1)}, f32[768]{0:T(1024)}, u32[]{:S(2)}) copy-start(f32[768]{0:T(1024)} %get-tuple-element.67) | copy-start | bytes 9220
  204.9 57.9 %copy-start.5 = (bf16[1,1,12,768]{3,1,2,0:T(2,128)(2,1)S(1)}, bf16[1,1,12,768]{3,1,2,0:T(2,128)(2,1)}, u32[]{:S(2)}) copy-start(bf16[1,1,12,768]{3,1,2,0:T(2,128)(2,1)} %get-tuple-element.59) | copy-start | bytes 55300
  205.1 62.4 %copy-start.3 = (bf16[1,768,3,8,8]{1,4,3,2,0:T(8,128)(2,1)}, bf16[1,768,3,8,8]{1,4,3,2,0:T(8,128)(2,1)S(1)}, u32[]{:S(2)}) copy-start(bf16[1,768,3,8,8]{1,4,3,2,0:T(8,128)(2,1)S(1)} %get-tuple-element.34) | copy-start | bytes 884740
  251.7 4.6 %collective-permute-start.8 = (bf16[1,768,3,1,8]{1,4,3,2,0:T(8,128)(2,1)S(1)}, bf16[1,768,3,1,8]{1,4,3,2,0:T(8,128)(2,1)S(1)}, u32[]{:S(2)}, u32[]{:S(2)}) collective-permute-start(bf16[1,768,3,1,8]{1,4,3,2,0:T(8,128)(2,1)S(1)} %get-tuple-element.50), channel_id=1, source_target_pairs={{0,1},{1,2},{2,3},{3,4},{4,5},{5,6},{6,7},{8,9},{9,10},{10,11},{11... | collective-permute-start | bytes 110600 | tf_op jit(solution)/shard_map/ppermute | solution.py:26
  253.8 5.3 %collective-permute-start.9 = (bf16[1,768,3,1,8]{1,4,3,2,0:T(8,128)(2,1)S(1)}, bf16[1,768,3,1,8]{1,4,3,2,0:T(8,128)(2,1)S(1)}, u32[]{:S(2)}, u32[]{:S(2)}) collective-permute-start(bf16[1,768,3,1,8]{1,4,3,2,0:T(8,128)(2,1)S(1)} %get-tuple-element.51), channel_id=1, source_target_pairs={{1,0},{2,1},{3,2},{4,3},{5,4},{6,5},{7,6},{9,8},{10,9},{11,10},{12... | collective-permute-start | bytes 110600 | tf_op jit(solution)/shard_map/ppermute | solution.py:27
  259.3 3.8 collective-permute-start.10
  261.6 5.3 %collective-permute-start.11 = (bf16[1,768,3,10,1]{1,4,3,2,0:T(2,128)(2,1)S(1)}, bf16[1,768,3,10,1]{1,4,3,2,0:T(2,128)(2,1)S(1)}, u32[]{:S(2)}, u32[]{:S(2)}) collective-permute-start(bf16[1,768,3,10,1]{1,4,3,2,0:T(2,128)(2,1)S(1)} %get-tuple-element.41), channel_id=1, source_target_pairs={{8,0},{16,8},{24,16},{9,1},{17,9},{25,17},{10,2},{18,10},{26,18},{... | collective-permute-start | bytes 138248 | tf_op jit(solution)/shard_map/ppermute | solution.py:27
  267.5 81.0 %copy-start.7 = (f32[768]{0:T(1024)S(1)}, f32[768]{0:T(1024)}, u32[]{:S(2)}) copy-start(f32[768]{0:T(1024)} %get-tuple-element.24) | copy-start | bytes 9220
  267.5 81.0 %copy-start.8 = (f32[768]{0:T(1024)S(1)}, f32[768]{0:T(1024)}, u32[]{:S(2)}) copy-start(f32[768]{0:T(1024)} %get-tuple-element.68) | copy-start | bytes 9220
  267.5 81.0 %copy-start.9 = (f32[768]{0:T(1024)S(1)}, f32[768]{0:T(1024)}, u32[]{:S(2)}) copy-start(f32[768]{0:T(1024)} %get-tuple-element.32) | copy-start | bytes 9220
  267.5 81.0 %copy-start.10 = (f32[768]{0:T(1024)S(1)}, f32[768]{0:T(1024)}, u32[]{:S(2)}) copy-start(f32[768]{0:T(1024)} %get-tuple-element.64) | copy-start | bytes 9220
  348.8 4.4 collective-permute-start.12
  350.9 5.3 %collective-permute-start.13 = (bf16[1,768,3,1,8]{1,4,3,2,0:T(8,128)(2,1)S(1)}, bf16[1,768,3,1,8]{1,4,3,2,0:T(8,128)(2,1)S(1)}, u32[]{:S(2)}, u32[]{:S(2)}) collective-permute-start(bf16[1,768,3,1,8]{1,4,3,2,0:T(8,128)(2,1)S(1)} %get-tuple-element.49), channel_id=1, source_target_pairs={{1,0},{2,1},{3,2},{4,3},{5,4},{6,5},{7,6},{9,8},{10,9},{11,10},{12... | collective-permute-start | bytes 110600 | tf_op jit(solution)/shard_map/ppermute | solution.py:27
  356.4 3.8 collective-permute-start.14
  358.7 5.3 %collective-permute-start.15 = (bf16[1,768,3,10,1]{1,4,3,2,0:T(2,128)(2,1)S(1)}, bf16[1,768,3,10,1]{1,4,3,2,0:T(2,128)(2,1)S(1)}, u32[]{:S(2)}, u32[]{:S(2)}) collective-permute-start(bf16[1,768,3,10,1]{1,4,3,2,0:T(2,128)(2,1)S(1)} %get-tuple-element.39), channel_id=1, source_target_pairs={{8,0},{16,8},{24,16},{9,1},{17,9},{25,17},{10,2},{18,10},{26,18},{... | collective-permute-start | bytes 138248 | tf_op jit(solution)/shard_map/ppermute | solution.py:27
  399.3 6.2 %collective-permute-start.16 = (bf16[1,768,3,1,8]{1,4,3,2,0:T(8,128)(2,1)S(1)}, bf16[1,768,3,1,8]{1,4,3,2,0:T(8,128)(2,1)S(1)}, u32[]{:S(2)}, u32[]{:S(2)}) collective-permute-start(bf16[1,768,3,1,8]{1,4,3,2,0:T(8,128)(2,1)S(1)} %get-tuple-element.46), channel_id=1, source_target_pairs={{0,1},{1,2},{2,3},{3,4},{4,5},{5,6},{6,7},{8,9},{9,10},{10,11},{11... | collective-permute-start | bytes 110600 | tf_op jit(solution)/shard_map/ppermute | solution.py:26
  403.5 5.3 %collective-permute-start.17 = (bf16[1,768,3,1,8]{1,4,3,2,0:T(8,128)(2,1)S(1)}, bf16[1,768,3,1,8]{1,4,3,2,0:T(8,128)(2,1)S(1)}, u32[]{:S(2)}, u32[]{:S(2)}) collective-permute-start(bf16[1,768,3,1,8]{1,4,3,2,0:T(8,128)(2,1)S(1)} %get-tuple-element.47), channel_id=1, source_target_pairs={{1,0},{2,1},{3,2},{4,3},{5,4},{6,5},{7,6},{9,8},{10,9},{11,10},{12... | collective-permute-start | bytes 110600 | tf_op jit(solution)/shard_map/ppermute | solution.py:27
  408.9 4.3 collective-permute-start.18
  411.6 5.3 %collective-permute-start.19 = (bf16[1,768,3,10,1]{1,4,3,2,0:T(2,128)(2,1)S(1)}, bf16[1,768,3,10,1]{1,4,3,2,0:T(2,128)(2,1)S(1)}, u32[]{:S(2)}, u32[]{:S(2)}) collective-permute-start(bf16[1,768,3,10,1]{1,4,3,2,0:T(2,128)(2,1)S(1)} %get-tuple-element.37), channel_id=1, source_target_pairs={{8,0},{16,8},{24,16},{9,1},{17,9},{25,17},{10,2},{18,10},{26,18},{... | collective-permute-start | bytes 138248 | tf_op jit(solution)/shard_map/ppermute | solution.py:27
  (11 other events, 351.9 us)
where the time goes:
time: 448 us; the launch traced here: 444 us
  blocking collectives  186 us (42%)
  matrix products  155 us (35%)
  starting transfers between devices  43.1 us (10%)
  waiting for transfers between devices  32.4 us (7%)
  local copies, waits for them, and re-layouts  18.8 us (4%)
  other arithmetic  7.07 us (2%)
    psum x4, blocking collectives, group_norm(): total_stats = lax.psum(local_stats, ('sh', 'sw'))  186 us
    conv_general_dilated x4, matrix products, causal_conv(): lax.conv_general_dilated(padded, weight, (1, 1, 1), 'VALID', dimension_nu...  139 us
    ppermute x10, waiting for transfers between devices, edge_exchange(): lax.ppermute(head, axis_name, [(i + 1, i) for i in range(n_dev - 1)])  32.1 us
    ppermute x10, starting transfers between devices, edge_exchange(): lax.ppermute(tail, axis_name, [(i, i + 1) for i in range(n_dev - 1)])  24.4 us
    ppermute x10, starting transfers between devices, edge_exchange(): lax.ppermute(head, axis_name, [(i + 1, i) for i in range(n_dev - 1)])  18.6 us
    conv_general_dilated x1, matrix products, upsample_conv(): lax.conv_general_dilated(cropped, weight[:, :, None], (1, 1, 1), 'VALID',...  15.1 us
  transfers between devices with their start and end apart: 20, of which 11 were waited for; matrix products, arithmetic and copies ran while one was open for 0% of the time, Pallas kernels for 0%

commit v1 on v0

v1 whole, which is shorter than its diff:
```python
import functools

import jax
import jax.numpy as jnp
from jax import lax
from jax.experimental import pallas as pl
from jax.experimental.pallas import tpu as pltpu
from jax.sharding import PartitionSpec as P

NUM_GROUPS = 32
GN_EPSILON = 1e-6
TILE = 256
LANES = 128
SUB = 8
SLOTS = 12
EXPLICIT = False
F32 = jnp.float32
BF16 = jnp.bfloat16
MESH = pl.DeviceIdType.MESH
VMEM_BYTES = 66 * 1000 * 1000
SIDES = ((0, (1, 0)), (1, (-1, 0)), (2, (0, 1)), (3, (0, -1)))
CORNERS = ((0, (1, 1)), (1, (1, -1)), (2, (-1, 1)), (3, (-1, -1)))


class Mxu:
    def __init__(self):
        self.count = [0, 0]
        self.staged = None

    def push(self, rhs, q, transpose=False, value_transpose=False):
        reg = self.count[q] % 2
        self.count[q] += 1
        if EXPLICIT:
            if transpose and value_transpose:
                pltpu.matmul_push_rhs(rhs.T, staging_register=reg, mxu_index=q)
            else:
                pltpu.matmul_push_rhs(rhs, staging_register=reg, mxu_index=q, transpose=transpose)
        else:
            self.staged = rhs.T if transpose else rhs
        return reg

    def acc(self, ref, lhs, reg):
        if EXPLICIT:
            pltpu.matmul_acc_lhs(ref, lhs, load_staged_rhs=reg)
        else:
            ref[...] += jnp.dot(lhs.astype(BF16), self.staged, preferred_element_type=F32)

    def more(self, ref, lhs):
        if EXPLICIT:
            pltpu.matmul_acc_lhs(ref, lhs)
        else:
            ref[...] += jnp.dot(lhs.astype(BF16), self.staged, preferred_element_type=F32)

    def pop(self, ref):
        if EXPLICIT:
            return pltpu.matmul_pop(ref)
        val = ref[...]
        ref[...] = jnp.zeros_like(val)
        return val


def acc_ref(q, rows):
    return pltpu.ACC(q)((rows, TILE), F32) if EXPLICIT else pltpu.VMEM((rows, TILE), F32)


def split3(v):
    hi = v.astype(BF16)
    rest = v - hi.astype(F32)
    mid = rest.astype(BF16)
    low = (rest - mid.astype(F32)).astype(BF16)
    return hi, mid, low


def rounded(v):
    return v.astype(BF16).astype(F32)


def kernel(n_sh, n_sw, dims, feat, lat, gain, shift, zyb, zbb, cb, zyw, zbw, upb, wconv, wup, out,
           ring, xs, rf, xf, hact, zy, zb, zf, zw, par, gm, sums, msg, peers, side_out, corner_out, side_in, corner_in,
           tsum, yout, ring_sem, stat_send, stat_recv, halo_send, halo_recv):
    n_chan, n_frame, n_row, n_col, n_lat = dims
    n_pos = n_row * n_col
    n_tile = n_chan // TILE
    n_dev = n_sh * n_sw
    n_conv = 4
    n_tap = 9
    zlane = n_chan
    wide = n_chan + LANES
    sh = lax.axis_index("sh")
    sw = lax.axis_index("sw")
    me = sw * n_sh + sh
    count = float((n_chan // NUM_GROUPS) * n_frame * n_pos * n_dev)
    mxu = Mxu()
    total = n_conv * n_tap + 3

    def conv_copy(conv, tap, kt, slot):
        return pltpu.make_async_copy(wconv.at[conv, kt, tap], ring.at[slot, kt], ring_sem.at[slot])

    def up_copy(kh, kw, slot):
        return pltpu.make_async_copy(wup.at[kh * 3 + kw], ring.at[slot, kw], ring_sem.at[slot])

    def wait_chunk(slot):
        pltpu.make_async_copy(wconv.at[0, pl.ds(0, 3), 0], ring.at[slot], ring_sem.at[slot]).wait()

    def refill(g):
        nxt = g + SLOTS
        slot = lax.rem(g, SLOTS)

        @pl.when(nxt < n_conv * n_tap)
        def _():
            conv = nxt // n_tap
            for kt in range(3):
                conv_copy(conv, nxt - conv * n_tap, kt, slot).start()

        @pl.when((nxt >= n_conv * n_tap) & (nxt < total))
        def _():
            for kw in range(3):
                up_copy(nxt - n_conv * n_tap, kw, slot).start()

    for g in range(SLOTS):
        for kt in range(3):
            conv_copy(g // n_tap, g % n_tap, kt, g).start()
    side_in[...] = jnp.zeros_like(side_in)
    corner_in[...] = jnp.zeros_like(corner_in)

    def peer(step):
        dev = lax.rem(me + step, n_dev)
        return {"sw": dev // n_sh, "sh": lax.rem(dev, n_sh)}

    barrier = pltpu.get_barrier_semaphore()

    def tell(step, carry):
        pl.semaphore_signal(barrier, inc=1, device_id=peer(step), device_id_type=MESH)
        return carry

    lax.fori_loop(1, n_dev, tell, 0)

    for b in range(2):
        for s in range(2):
            for row, ref in enumerate((gain, shift, zyb, zbb, cb)):
                par[2 * b + s, row:row + 1, :] = ref[b, s:s + 1, :]
    zw[...] = jnp.zeros_like(zw)
    for which, ref in enumerate((zyw, zbw)):
        for b in range(2):
            for k in range(n_lat):
                pair = ref[b, k].astype(F32)
                for s in range(2):
                    zw[2 * b + s, which, k:k + 1, :] = pair[s:s + 1, :]
    zf[...] = jnp.zeros_like(zf)
    zf[0:n_frame * n_pos, 0:n_lat] = lat[...].astype(F32)
    chan_iota = lax.broadcasted_iota(jnp.int32, (TILE, TILE), 0)
    group_iota = lax.broadcasted_iota(jnp.int32, (TILE, TILE), 1) * (n_chan // NUM_GROUPS)
    for n in range(n_tile):
        off = chan_iota + n * TILE - group_iota
        gm[n] = jnp.where((off >= 0) & (off < n_chan // NUM_GROUPS), 1.0, 0.0).astype(BF16)
    start = feat[...].astype(F32)
    rf[...] = start
    xf[...] = start
    sums[0:SUB, :] = jnp.sum(start.reshape(-1, SUB, n_chan), axis=0)
    sums[SUB:, :] = jnp.sum(jnp.square(start).reshape(-1, SUB, n_chan), axis=0)
    sub_iota = lax.broadcasted_iota(jnp.int32, (SUB, n_chan), 0)

    def gather_rows(ref, at, step, n, cols):
        lanes = cols.stop - cols.start
        iota = lax.broadcasted_iota(jnp.int32, (SUB, lanes), 0)
        piece = jnp.zeros((SUB, lanes), F32)
        for i in range(n):
            row = jnp.broadcast_to(ref[at + i * step:at + i * step + 1, cols], (SUB, lanes))
            piece = jnp.where(iota == i, row, piece)
        return piece.astype(BF16)

    def stage(ref, lane0, lanes):
        cols = slice(0, lanes)
        put = slice(lane0, lane0 + lanes)
        for t in range(n_frame):
            base = t * n_pos
            side_out[0, t, :, put] = ref[base + n_pos - n_col:base + n_pos, cols].astype(BF16)
            side_out[1, t, :, put] = ref[base:base + n_col, cols].astype(BF16)
            side_out[2, t, :, put] = gather_rows(ref, base + n_col - 1, n_col, n_row, cols)
            side_out[3, t, :, put] = gather_rows(ref, base, n_col, n_row, cols)
        for d, at in enumerate((n_pos - 1, n_pos - n_col, n_col - 1, 0)):
            corner_out[d, :, put] = gather_rows(ref, at, n_pos, n_frame, cols)

    stage(zf, zlane, LANES)

    def inside(row, col):
        ok = None
        for step, pos, n in ((row, sh, n_sh), (col, sw, n_sw)):
            if step == 0:
                continue
            one = pos + step < n if step > 0 else pos + step >= 0
            ok = one if ok is None else ok & one
        return ok

    def halo_copies(slot):
        found = []
        for kind, (outs, ins, steps) in enumerate(((side_out, side_in, SIDES), (corner_out, corner_in, CORNERS))):
            for d, (row, col) in steps:
                copy = pltpu.make_async_remote_copy(
                    src_ref=outs.at[d], dst_ref=ins.at[slot, d], send_sem=halo_send.at[kind * 4 + d],
                    recv_sem=halo_recv.at[slot, kind * 4 + d], device_id={"sh": sh + row, "sw": sw + col}, device_id_type=MESH)
                found.append((copy, inside(row, col), inside(-row, -col)))
        return found

    def halo_start(slot):
        for copy, to, _ in halo_copies(slot):
            @pl.when(to)
            def _():
                copy.start()

    def halo_wait(slot):
        for copy, to, source in halo_copies(slot):
            @pl.when(source)
            def _():
                copy.wait_recv()

            @pl.when(to)
            def _():
                copy.wait_send()

    def stat_copy(slot, step):
        return pltpu.make_async_remote_copy(
            src_ref=msg, dst_ref=peers.at[slot, me], send_sem=stat_send, recv_sem=stat_recv.at[slot],
            device_id=peer(step), device_id_type=MESH)

    def stat_all(slot):
        part = peers.at[slot, pl.ds(0, n_dev - 1)]
        return pltpu.make_async_remote_copy(
            src_ref=part, dst_ref=part, send_sem=stat_send, recv_sem=stat_recv.at[slot], device_id=peer(1), device_id_type=MESH)

    def stats_start(slot, aux):
        for k in range(n_tile):
            reg = mxu.push(gm[k], 0)
            for i, piece in enumerate(split3(sums[:, k * TILE:(k + 1) * TILE])):
                if i == 0:
                    mxu.acc(aux, piece, reg)
                else:
                    mxu.more(aux, piece)
        got = mxu.pop(aux)[:, 0:LANES]
        mine = jnp.concatenate([jnp.sum(got[0:SUB], axis=0, keepdims=True), jnp.sum(got[SUB:], axis=0, keepdims=True)], axis=0)
        msg[...] = mine
        peers[slot, me] = mine

        def go(step, carry):
            stat_copy(slot, step).start()
            return carry

        lax.fori_loop(1, n_dev, go, 0)

    def stats_finish(slot, aux):
        both = stat_all(slot)
        both.wait_recv()
        both.wait_send()
        tot = jnp.sum(peers[slot], axis=0)
        mean = tot[0:1] / count
        var = jnp.maximum(tot[1:2] / count - jnp.square(mean), 0.0)
        inv = lax.rsqrt(var + GN_EPSILON)
        rows = lax.broadcasted_iota(jnp.int32, (2 * SUB, LANES), 0)
        left = jnp.where(rows == 0, mean, jnp.where(rows == 1, inv, 0.0))
        lhs = jnp.concatenate([left, jnp.zeros_like(left)], axis=1)
        pieces = split3(lhs)
        found = []
        for n in range(n_tile):
            reg = mxu.push(gm[n], n % 2, transpose=True)
            for i, piece in enumerate(pieces):
                if i == 0:
                    mxu.acc(aux[n], piece, reg)
                else:
                    mxu.more(aux[n], piece)
        for n in range(n_tile):
            found.append(mxu.pop(aux[n]))
        whole = jnp.concatenate(found, axis=1)
        return whole[0:1], whole[1:2]

    def latent_maps(conv, accs):
        n_own = n_frame * n_pos
        zeros = jnp.zeros((TILE - 2 * SUB, TILE), BF16)
        for which, (dst, row) in enumerate(((zy, 2), (zb, 3))):
            for n in range(n_tile):
                q = n % 2
                cols = slice(n * TILE, (n + 1) * TILE)
                w = jnp.concatenate([zw[conv, which, :, cols].astype(BF16), zeros], axis=0)
                bias = par[conv, row:row + 1, cols]
                reg = mxu.push(w, q)
                mxu.acc(accs[q][0][2], zf[0:n_own, :], reg)
                mxu.more(accs[q][0][1], zf[n_own:, :])
                dst[0:n_own, cols] = mxu.pop(accs[q][0][2]) + bias
                dst[n_own:, cols] = mxu.pop(accs[q][0][1]) + bias

    halo_flags = [inside(-row, -col) for _, (row, col) in SIDES] + [inside(-row, -col) for _, (row, col) in CORNERS]

    def halo_values(slot, q):
        if q < 4 * n_frame:
            return side_in[slot, q // n_frame, q % n_frame, :, 0:n_chan].astype(F32), halo_flags[q // n_frame]
        return corner_in[slot, q - 4 * n_frame, :, 0:n_chan].astype(F32), halo_flags[4 + q - 4 * n_frame]

    n_side = n_frame * SUB

    def put_rows(t, at, mid, before, after):
        xs[1, t, pl.ds(at, SUB), :] = mid
        xs[0, t, pl.ds(at, SUB), :] = jnp.where(sub_iota == 0, before, pltpu.roll(mid, 1, axis=0))
        xs[2, t, pl.ds(at, SUB), :] = jnp.where(sub_iota == SUB - 1, after, pltpu.roll(mid, SUB - 1, axis=0))

    def build(slot, value_fn):
        for q in range(4 * n_frame + 4):
            v, flag = halo_values(slot, q)
            hact[q * SUB:(q + 1) * SUB, :] = jnp.where(flag, value_fn(v, n_frame * n_pos + q * SUB), 0.0)
        for t in range(n_frame):
            for at, side, corner in ((0, 0, 0), ((n_row + 1) * SUB, 1, 2)):
                mid = hact[side * n_side + t * SUB:side * n_side + (t + 1) * SUB, :]
                c0 = 4 * n_side + corner * SUB + t
                put_rows(t, at, mid, hact[c0:c0 + 1, :], hact[c0 + SUB:c0 + SUB + 1, :])

        def rows(g, carry):
            at = pl.multiple_of(g * SUB, SUB)
            t = g // n_row
            mid = value_fn(rf[pl.ds(at, SUB), :], at)
            put_rows(t, pl.multiple_of((g - t * n_row + 1) * SUB, SUB), mid, hact[pl.ds(2 * n_side + g, 1), :], hact[pl.ds(3 * n_side + g, 1), :])
            return carry

        lax.fori_loop(0, n_frame * n_row, rows, 0, unroll=4)

    def convs(*accs_flat):
        aux = accs_flat[:3]
        conv_acc = accs_flat[15:]
        accs_flat = accs_flat[:15]
        accs = [[dict(zip((0, 1, 2), accs_flat[3 + 6 * q + 3 * i:6 + 6 * q + 3 * i])) for i in range(2)] for q in range(2)]
        for ref in accs_flat:
            mxu.pop(ref)
        pl.semaphore_wait(barrier, n_dev - 1)

        def one_conv(conv, carry):
            slot = lax.rem(conv, 2)
            stats_start(slot, aux[0])
            stage(rf, 0, n_chan)
            halo_start(slot)
            halo_wait(slot)

            @pl.when(conv == 0)
            def _():
                n_own = n_frame * n_pos
                for q in range(4 * n_frame):
                    zf[n_own + q * SUB:n_own + (q + 1) * SUB, 0:LANES] = side_in[slot, q // n_frame, q % n_frame, :, zlane:wide].astype(F32)
                for q in range(4):
                    at = n_own + (4 * n_frame + q) * SUB
                    zf[at:at + SUB, 0:LANES] = corner_in[slot, q, :, zlane:wide].astype(F32)

            latent_maps(conv, accs)
            mean, inv = stats_finish(slot, aux)
            scale = inv * par[conv, 0:1, :]
            offset = par[conv, 1:2, :]

            def act(v, at):
                normed = (v - mean) * scale + offset
                mixed = normed * zy[pl.ds(at, SUB), :] + zb[pl.ds(at, SUB), :]
                return rounded(mixed / (1.0 + jnp.exp(-mixed)))

            build(slot, act)

            def tap(p, carry):
                g = conv * n_tap + p
                ring_slot = lax.rem(g, SLOTS)
                kh = p // 3
                kw = p - 3 * kh
                wait_chunk(ring_slot)
                at = pl.multiple_of(kh * SUB, SUB)
                for kt in (2, 1, 0):
                    lhs = xs[kw, 0:kt + 1, pl.ds(at, n_pos), :].reshape((kt + 1) * n_pos, n_chan).astype(BF16)
                    conv_acc[kt][...] += lax.dot_general(lhs, ring[ring_slot, kt], (((1,), (1,)), ((), ())), preferred_element_type=F32)
                refill(g)
                return carry

            for ref in conv_acc:
                ref[...] = jnp.zeros_like(ref)
            lax.fori_loop(0, n_tap, tap, 0)

            odd = lax.rem(conv, 2) == 1
            for n in range(n_tile):
                cols = slice(n * TILE, (n + 1) * TILE)
                r2, r1, r0 = [conv_acc[kt][:, cols] for kt in (2, 1, 0)]
                bias = par[conv, 4:5, cols]
                s1 = jnp.zeros((SUB, TILE), F32)
                s2 = jnp.zeros((SUB, TILE), F32)
                for t in range(n_frame):
                    early = max(t - 1, 0)
                    rows = slice(t * n_pos, (t + 1) * n_pos)
                    y = rounded(r2[rows] + r1[early * n_pos:(early + 1) * n_pos] + r0 + bias)
                    old = xf[rows, cols]
                    x = jnp.where(odd, rounded(old + y), y)
                    xf[rows, cols] = jnp.where(odd, x, old)
                    rf[rows, cols] = x
                    s1 += jnp.sum(x.reshape(-1, SUB, TILE), axis=0)
                    s2 += jnp.sum(jnp.square(x).reshape(-1, SUB, TILE), axis=0)
                sums[0:SUB, cols] = s1
                sums[SUB:, cols] = s2
            return carry

        lax.fori_loop(0, n_conv, one_conv, 0)

    specs = [acc_ref(0, 2 * SUB), acc_ref(1, 2 * SUB), acc_ref(0, 2 * SUB)]
    for q in range(2):
        for _ in range(2):
            specs += [acc_ref(q, (kt + 1) * n_pos) for kt in range(3)]
    specs += [pltpu.VMEM(((kt + 1) * n_pos, n_chan), F32) for kt in range(3)]
    pl.run_scoped(convs, *specs)

    stage(rf, 0, n_chan)
    last = n_conv % 2
    halo_start(last)
    halo_wait(last)
    build(last, lambda v, at: v)
    n_up = (n_row + 1) * n_col

    def upsample(*accs_flat):
        accs = [accs_flat[3 * q:3 * q + 3] for q in range(2)]
        for ref in accs_flat:
            mxu.pop(ref)
        for kh in range(3):
            g = n_conv * n_tap + kh
            ring_slot = g % SLOTS
            wait_chunk(ring_slot)
            at = SUB * min(kh, 1)
            for n in range(n_tile):
                q = (kh * n_tile + n) % 2
                cols = slice(n * TILE, (n + 1) * TILE)
                for kw, uses in ((0, ((0, 0), (1, 2))), (2, ((1, 0), (2, 2))), (1, ((1, 1),))):
                    for k in range(n_tile):
                        ks = slice(k * TILE, (k + 1) * TILE)
                        reg = mxu.push(ring[ring_slot, kw, cols, ks], q, transpose=True)
                        for i, (shifted, group) in enumerate(uses):
                            lhs = xs[shifted, :, at:at + n_up, ks].reshape(n_frame * n_up, TILE)
                            if i == 0:
                                mxu.acc(accs[q][group], lhs, reg)
                            else:
                                mxu.more(accs[q][group], lhs)
                first, last_, both = mxu.pop(accs[q][0]), mxu.pop(accs[q][2]), mxu.pop(accs[q][1])
                tsum[kh, 0, :, cols] = first + both
                tsum[kh, 1, :, cols] = last_ + both

    pl.run_scoped(upsample, *[acc_ref(q, n_frame * n_up) for q in range(2) for _ in range(3)])

    bias = upb[...]
    n_up_rows = n_row + 1

    def finish(g, carry):
        t = g // n_row
        i = g - t * n_row
        here = t * n_up + i * SUB
        for a in range(2):
            for b in range(2):
                v = bias
                for kh in range(3):
                    down = SUB if (a == 1 and kh != 1) else 0
                    v = v + tsum[kh, b, pl.ds(pl.multiple_of(here + down, SUB), SUB), :]
                for j in range(n_chan // LANES):
                    yout[a, j, pl.ds(b, SUB, stride=2), :] = v[:, j * LANES:(j + 1) * LANES]
            for j in range(n_chan // LANES):
                out[t, 2 * i + a, :, j * LANES:(j + 1) * LANES] = yout[a, j].astype(BF16)
        return carry

    lax.fori_loop(0, n_frame * n_row, finish, 0)


XLU_TILES = ()


def solution(mesh):
    n_sh = mesh.shape["sh"]
    n_sw = mesh.shape["sw"]
    n_dev = n_sh * n_sw

    def local_step(features, latent, gn_gain, gn_bias, zy_weight, zy_bias, zb_weight, zb_bias, conv_weight, conv_bias, up_weight, up_bias):
        _, n_chan, n_frame, n_row, n_col = features.shape
        n_lat = latent.shape[1]
        n_pos = n_row * n_col
        n_own = n_frame * n_pos
        n_halo = (4 * n_frame + 4) * SUB
        feat = jnp.transpose(features, (0, 2, 3, 4, 1)).reshape(n_own, n_chan)
        lat = jnp.transpose(latent, (0, 2, 3, 4, 1)).reshape(n_own, n_lat)
        wconv = jnp.transpose(conv_weight, (0, 1, 4, 5, 6, 2, 3)).reshape(4, 3, 9, n_chan, n_chan)
        wup = jnp.transpose(up_weight, (2, 3, 0, 1)).reshape(9, n_chan, n_chan)
        zyw = jnp.transpose(zy_weight, (0, 2, 1, 3))
        zbw = jnp.transpose(zb_weight, (0, 2, 1, 3))
        vmem = pl.BlockSpec(memory_space=pltpu.VMEM)
        hbm = pl.BlockSpec(memory_space=pl.ANY)
        wide = n_chan + LANES
        y = pl.pallas_call(
            functools.partial(kernel, n_sh, n_sw, (n_chan, n_frame, n_row, n_col, n_lat)),
            out_shape=jax.ShapeDtypeStruct((n_frame, 2 * n_row, 2 * n_col, n_chan), BF16),
            in_specs=[vmem] * 10 + [hbm] * 2,
            out_specs=vmem,
            scratch_shapes=[
                pltpu.VMEM((SLOTS, 3, n_chan, n_chan), BF16),
                pltpu.VMEM((3, n_frame, (n_row + 2) * SUB, n_chan), F32),
                pltpu.VMEM((n_own, n_chan), F32),
                pltpu.VMEM((n_own, n_chan), F32),
                pltpu.VMEM((n_halo, n_chan), F32),
                pltpu.VMEM((n_own + n_halo, n_chan), F32),
                pltpu.VMEM((n_own + n_halo, n_chan), F32),
                pltpu.VMEM((n_own + n_halo, TILE), F32),
                pltpu.VMEM((4, 2, 2 * SUB, n_chan), F32),
                pltpu.VMEM((4, SUB, n_chan), F32),
                pltpu.VMEM((n_chan // TILE, TILE, TILE), BF16),
                pltpu.VMEM((2 * SUB, n_chan), F32),
                pltpu.VMEM((2, LANES), F32),
                pltpu.VMEM((2, n_dev, 2, LANES), F32),
                pltpu.VMEM((4, n_frame, SUB, wide), BF16),
                pltpu.VMEM((4, SUB, wide), BF16),
                pltpu.VMEM((2, 4, n_frame, SUB, wide), BF16),
                pltpu.VMEM((2, 4, SUB, wide), BF16),
                pltpu.VMEM((3, 2, n_frame * (n_row + 1) * n_col, n_chan), F32),
                pltpu.VMEM((2, n_chan // LANES, 2 * n_col, LANES), F32),
                pltpu.SemaphoreType.DMA((SLOTS,)),
                pltpu.SemaphoreType.DMA,
                pltpu.SemaphoreType.DMA((2,)),
                pltpu.SemaphoreType.DMA((8,)),
                pltpu.SemaphoreType.DMA((2, 8)),
            ],
            compiler_params=pltpu.CompilerParams(collective_id=0, has_side_effects=True, vmem_limit_bytes=VMEM_BYTES),
        )(feat, lat, gn_gain, gn_bias, zy_bias, zb_bias, conv_bias, zyw, zbw, up_bias.reshape(1, n_chan), wconv, wup)
        return jnp.transpose(y.reshape(1, n_frame, 2 * n_row, 2 * n_col, n_chan), (0, 4, 1, 2, 3))

    data_spec = P("dp", None, None, "sh", "sw")
    return jax.shard_map(local_step, mesh=mesh, in_specs=(data_spec, data_spec) + (P(),) * 10, out_specs=data_spec, check_vma=False)
```

time: 448 us -> 99.9 us (0.22)
  blocking collectives: 186 us -> 0 us
  matrix products: 155 us -> 0 us
  Pallas kernels: 0 us -> 96.1 us
  starting transfers between devices: 43.1 us -> 0 us
  waiting for transfers between devices: 32.4 us -> 0 us
  local copies, waits for them, and re-layouts: 18.8 us -> 3.63 us
  other arithmetic: 7.07 us -> 0 us
    psum x4 -> x0, blocking collectives: 186 us -> none  [group_norm(): total_stats = lax.psum(local_stats, ('sh', 'sw'))]
    conv_general_dilated x5 -> x0, matrix products: 154 us -> none  [the longest x4 139 us: causal_conv(): lax.conv_general_dilated(padded, weight, (1, 1, 1), 'VALID', dimension_nu...]
    pallas_call x0 -> x1, Pallas kernels: none -> 96.1 us  [local_step(): pl.pallas_call(functools.partial(kernel, n_sh, n_sw, (n_chan, n_frame, n_...]
    ppermute x20 -> x0, starting transfers between devices: 43.1 us -> none  [the longest x10 24.4 us: edge_exchange(): lax.ppermute(tail, axis_name, [(i, i + 1) for i in range(n_dev - 1)])]
    ppermute x20 -> x0, waiting for transfers between devices: 32.4 us -> none  [the longest x10 32.1 us: edge_exchange(): lax.ppermute(head, axis_name, [(i + 1, i) for i in range(n_dev - 1)])]
    broadcast_in_dim x5 -> x0, local copies, waits for them, and re-layouts: 8 us -> none  [upsample_conv(): upsampled = jnp.repeat(jnp.repeat(bordered, 2, axis=3), 2, axis=4)]
    slice x10 -> x0, local copies, waits for them, and re-layouts: 5.97 us -> none  [the longest x1 1.6 us: local_step(): zb_weight[block, slot]]
  transfers between devices with their start and end apart: 20 -> 0, of which waited for: 11 -> 0; matrix products, arithmetic and copies ran while one was open for 0% -> 0% of each run, Pallas kernels for 0% -> 0%
where the time goes in v1:
time: 99.9 us; the launch traced here: 99.8 us
  Pallas kernels  96.1 us (96%)
  local copies, waits for them, and re-layouts  3.63 us (4%)
    pallas_call x1, Pallas kernels, local_step(): pl.pallas_call(functools.partial(kernel, n_sh, n_sw, (n_chan, n_frame, n_...  96.1 us
    unnamed x1, local copies, waits for them, and re-layouts  2.37 us

profile of v1, /device:TPU:97, one launch (start us, length us, event | category | flops | bytes accessed | tf_op | source)
XLA Modules:
  0.0 99.8 jit_solution(17191297896755884360)
XLA Ops:
  0.0 1.3 %reshape.20.upb = f32[1,768]{1,0:T(1,128)} reshape(f32[768]{0:T(1024)} %param.23) | data formatting | bytes 6144 | tf_op jit(solution)/shard_map/reshape | solution.py:520
  1.3 96.1 %shard_map.118 = bf16[3,16,16,768]{3,2,1,0:T(8,128)(2,1)} custom-call(bf16[192,768]{1,0:T(8,128)(2,1)} %bitcast.19, bf16[192,12]{1,0:T(8,128)(2,1)} %bitcast.22, f32[2,2,768]{2,1,0:T(2,128)} %gain.1, f32[2,2,768]{2,1,0:T(2,128)} %shift.1, f32[2,2,768]{2,1,0:T(2,128)} %zyb.1, f32[2,2,768]{2,1,0:T(2,128)} %zbb.1, f32[2,2,768]{2,1,0:T(2,128)} %cb.1, ...), custom_call_target="tpu_custom_call" | custom-call | tf_op jit(solution)/shard_map/pallas_call | solution.py:487
  97.4 2.4 %copy.14 = bf16[1,768,3,16,16]{1,4,3,2,0:T(8,128)(2,1)} copy(bf16[1,768,3,16,16]{1,4,3,2,0:T(8,128)(2,1)} %bitcast.18) | data formatting | bytes 2359296

commit v2 on v1

v2 whole, which is shorter than its diff:
```python
import functools

import jax
import jax.numpy as jnp
from jax import lax
from jax.experimental import pallas as pl
from jax.experimental.pallas import tpu as pltpu
from jax.sharding import PartitionSpec as P

NUM_GROUPS = 32
GN_EPSILON = 1e-6
TILE = 256
LANES = 128
SUB = 8
SLOTS = 12
GROUP = 3
F32 = jnp.float32
BF16 = jnp.bfloat16
MESH = pl.DeviceIdType.MESH
VMEM_BYTES = 66 * 1000 * 1000
SIDES = ((0, (1, 0)), (1, (-1, 0)), (2, (0, 1)), (3, (0, -1)))
CORNERS = ((0, (1, 1)), (1, (1, -1)), (2, (-1, 1)), (3, (-1, -1)))


def split3(v):
    hi = v.astype(BF16)
    rest = v - hi.astype(F32)
    mid = rest.astype(BF16)
    low = (rest - mid.astype(F32)).astype(BF16)
    return hi, mid, low


def rounded(v):
    return v.astype(BF16).astype(F32)


def dot(a, b):
    return jnp.dot(a, b, preferred_element_type=F32)


def dot_nt(a, b):
    return lax.dot_general(a, b, (((1,), (1,)), ((), ())), preferred_element_type=F32)


def peer_steps(n_sh, n_sw):
    cores = 2 if n_sh % 2 == 0 else 1
    n_x = n_sh // cores
    steps = [(x, y, c) for x in range(n_x) for y in range(n_sw) for c in range(cores)][1:]
    return cores, n_x, sorted(steps, key=lambda s: -(min(s[0], n_x - s[0]) + min(s[1], n_sw - s[1])))


def kernel(n_sh, n_sw, dims, feat, lat, gain, shift, zyb, zbb, cb, zyw, zbw, upb, wconv, wup, out,
           ring, xs, rf, xf, hact, zy, zb, zf, zw, par, gm, gmt, sums, msg, peers, side_out, corner_out, side_in, corner_in,
           acc_0, acc_1, acc_2, tsum, yout, ring_sem, stat_send, stat_recv, halo_send, halo_recv):
    n_chan, n_frame, n_row, n_col, n_lat = dims
    n_pos = n_row * n_col
    n_own = n_frame * n_pos
    n_dev = n_sh * n_sw
    n_conv = 4
    n_tap = 9
    zlane = n_chan
    wide = n_chan + LANES
    sh = lax.axis_index("sh")
    sw = lax.axis_index("sw")
    me = sw * n_sh + sh
    per_group = n_chan // NUM_GROUPS
    count = float(per_group * n_own * n_dev)
    total = n_conv * n_tap + 3
    accs = (acc_0, acc_1, acc_2)

    def conv_copy(conv, tap, kt, slot):
        return pltpu.make_async_copy(wconv.at[conv, kt, tap], ring.at[slot, kt], ring_sem.at[slot])

    def up_copy(kh, kw, slot):
        return pltpu.make_async_copy(wup.at[kh * 3 + kw], ring.at[slot, kw], ring_sem.at[slot])

    def wait_chunk(slot):
        pltpu.make_async_copy(wconv.at[0, pl.ds(0, 3), 0], ring.at[slot], ring_sem.at[slot]).wait()

    def refill(g):
        nxt = g + SLOTS
        slot = lax.rem(g, SLOTS)

        @pl.when(nxt < n_conv * n_tap)
        def _():
            conv = nxt // n_tap
            for kt in range(3):
                conv_copy(conv, nxt - conv * n_tap, kt, slot).start()

        @pl.when((nxt >= n_conv * n_tap) & (nxt < total))
        def _():
            for kw in range(3):
                up_copy(nxt - n_conv * n_tap, kw, slot).start()

    cores, n_x, steps = peer_steps(n_sh, n_sw)
    chip = sh // cores
    core = sh - chip * cores

    def peer(step):
        return {"sh": lax.rem(chip + step[0], n_x) * cores + lax.rem(core + step[2], cores), "sw": lax.rem(sw + step[1], n_sw)}

    barrier = pltpu.get_barrier_semaphore()
    for step in steps:
        pl.semaphore_signal(barrier, inc=1, device_id=peer(step), device_id_type=MESH)
    for g in range(SLOTS):
        for kt in range(3):
            conv_copy(g // n_tap, g % n_tap, kt, g).start()

    def gather_rows(ref, at, step, n, cols):
        lanes = cols.stop - cols.start
        iota = lax.broadcasted_iota(jnp.int32, (SUB, lanes), 0)
        piece = jnp.zeros((SUB, lanes), F32)
        for i in range(n):
            row = jnp.broadcast_to(ref[at + i * step:at + i * step + 1, cols], (SUB, lanes))
            piece = jnp.where(iota == i, row, piece)
        return piece.astype(BF16)

    def stage(ref, lane0, lanes):
        cols = slice(0, lanes)
        put = slice(lane0, lane0 + lanes)
        for t in range(n_frame):
            base = t * n_pos
            side_out[0, t, :, put] = ref[base + n_pos - n_col:base + n_pos, cols].astype(BF16)
            side_out[1, t, :, put] = ref[base:base + n_col, cols].astype(BF16)
            side_out[2, t, :, put] = gather_rows(ref, base + n_col - 1, n_col, n_row, cols)
            side_out[3, t, :, put] = gather_rows(ref, base, n_col, n_row, cols)
        for d, at in enumerate((n_pos - 1, n_pos - n_col, n_col - 1, 0)):
            corner_out[d, :, put] = gather_rows(ref, at, n_pos, n_frame, cols)

    def inside(row, col):
        ok = None
        for step, pos, n in ((row, sh, n_sh), (col, sw, n_sw)):
            if step == 0:
                continue
            one = pos + step < n if step > 0 else pos + step >= 0
            ok = one if ok is None else ok & one
        return ok

    def halo_copies(slot):
        found = []
        for kind, (outs, ins, ways) in enumerate(((side_out, side_in, SIDES), (corner_out, corner_in, CORNERS))):
            for d, (row, col) in ways:
                copy = pltpu.make_async_remote_copy(
                    src_ref=outs.at[d], dst_ref=ins.at[slot, d], send_sem=halo_send.at[kind * 4 + d],
                    recv_sem=halo_recv.at[slot, kind * 4 + d], device_id={"sh": sh + row, "sw": sw + col}, device_id_type=MESH)
                found.append((copy, inside(row, col), inside(-row, -col)))
        return found

    def halo_start(slot):
        for copy, to, _ in halo_copies(slot):
            @pl.when(to)
            def _():
                copy.start()

    def halo_wait(slot):
        for copy, to, source in halo_copies(slot):
            @pl.when(source)
            def _():
                copy.wait_recv()

            @pl.when(to)
            def _():
                copy.wait_send()

    def stat_copy(slot, step):
        return pltpu.make_async_remote_copy(
            src_ref=msg, dst_ref=peers.at[slot, me], send_sem=stat_send, recv_sem=stat_recv.at[slot],
            device_id=peer(step), device_id_type=MESH)

    def stat_all(slot):
        part = peers.at[slot, pl.ds(0, n_dev - 1)]
        return pltpu.make_async_remote_copy(
            src_ref=part, dst_ref=part, send_sem=stat_send, recv_sem=stat_recv.at[slot], device_id=peer(steps[0]), device_id_type=MESH)

    def group_sums(slot, values):
        got = dot(jnp.concatenate(split3(values), axis=0), gm[...])
        rows = got[0:2 * SUB] + got[2 * SUB:4 * SUB] + got[4 * SUB:6 * SUB]
        mine = jnp.concatenate([jnp.sum(rows[0:SUB], axis=0, keepdims=True), jnp.sum(rows[SUB:], axis=0, keepdims=True)], axis=0)
        msg[...] = mine
        peers[slot, me] = mine

    def stats_send(slot):
        for step in steps:
            stat_copy(slot, step).start()

    def stats_finish(slot):
        both = stat_all(slot)
        both.wait_recv()
        both.wait_send()
        tot = jnp.sum(peers[slot], axis=0)
        mean = tot[0:1] / count
        var = jnp.maximum(tot[1:2] / count - jnp.square(mean), 0.0)
        inv = lax.rsqrt(var + GN_EPSILON)
        rows = lax.broadcasted_iota(jnp.int32, (SUB, LANES), 0)
        lhs = jnp.where(rows == 0, mean, jnp.where(rows == 1, inv, 0.0))
        got = dot(jnp.concatenate(split3(lhs), axis=0), gmt[...])
        whole = got[0:SUB] + got[SUB:2 * SUB] + got[2 * SUB:3 * SUB]
        return whole[0:1], whole[1:2]

    def latent_maps(conv):
        got = dot(zf[...].astype(BF16), zw[conv])
        zy[...] = got[:, 0:n_chan] + par[conv, 2:3, :]
        zb[...] = got[:, n_chan:] + par[conv, 3:4, :]

    halo_flags = [inside(-row, -col) for _, (row, col) in SIDES] + [inside(-row, -col) for _, (row, col) in CORNERS]

    def halo_values(slot, q):
        if q < 4 * n_frame:
            return side_in[slot, q // n_frame, q % n_frame, :, 0:n_chan].astype(F32), halo_flags[q // n_frame]
        return corner_in[slot, q - 4 * n_frame, :, 0:n_chan].astype(F32), halo_flags[4 + q - 4 * n_frame]

    n_side = n_frame * SUB
    sub_iota = lax.broadcasted_iota(jnp.int32, (SUB, n_chan), 0)

    def put_rows(t, at, mid, before, after):
        xs[1, t, pl.ds(at, SUB), :] = mid
        xs[0, t, pl.ds(at, SUB), :] = jnp.where(sub_iota == 0, before, pltpu.roll(mid, 1, axis=0))
        xs[2, t, pl.ds(at, SUB), :] = jnp.where(sub_iota == SUB - 1, after, pltpu.roll(mid, SUB - 1, axis=0))

    def build(slot, value_fn):
        for q in range(4 * n_frame + 4):
            v, flag = halo_values(slot, q)
            hact[q * SUB:(q + 1) * SUB, :] = jnp.where(flag, value_fn(v, n_own + q * SUB), 0.0)
        for t in range(n_frame):
            for at, side, corner in ((0, 0, 0), ((n_row + 1) * SUB, 1, 2)):
                mid = hact[side * n_side + t * SUB:side * n_side + (t + 1) * SUB, :]
                c0 = 4 * n_side + corner * SUB + t
                put_rows(t, at, mid, hact[c0:c0 + 1, :], hact[c0 + SUB:c0 + SUB + 1, :])

        def rows(g, carry):
            at = pl.multiple_of(g * SUB, SUB)
            t = g // n_row
            mid = value_fn(rf[pl.ds(at, SUB), :], at)
            put_rows(t, pl.multiple_of((g - t * n_row + 1) * SUB, SUB), mid, hact[pl.ds(2 * n_side + g, 1), :], hact[pl.ds(3 * n_side + g, 1), :])
            return carry

        lax.fori_loop(0, n_frame * n_row, rows, 0, unroll=4)

    for ref, g_dim, c_dim in ((gm, 1, 0), (gmt, 0, 1)):
        off = lax.broadcasted_iota(jnp.int32, ref.shape, c_dim) - lax.broadcasted_iota(jnp.int32, ref.shape, g_dim) * per_group
        ref[...] = jnp.where((off >= 0) & (off < per_group), 1.0, 0.0).astype(BF16)
    start = feat[...].astype(F32)
    rf[...] = start
    xf[...] = start
    group_sums(0, jnp.concatenate([jnp.sum(start.reshape(-1, SUB, n_chan), axis=0), jnp.sum(jnp.square(start).reshape(-1, SUB, n_chan), axis=0)], axis=0))
    pl.semaphore_wait(barrier, n_dev - 1)
    stats_send(0)
    zf[...] = jnp.zeros_like(zf)
    zf[0:n_own, 0:n_lat] = lat[...].astype(F32)
    stage(zf, zlane, LANES)
    stage(rf, 0, n_chan)
    halo_start(0)
    for b in range(2):
        for s in range(2):
            for row, ref in enumerate((gain, shift, zyb, zbb, cb)):
                par[2 * b + s, row:row + 1, :] = ref[b, s:s + 1, :]
    for which, ref in enumerate((zyw, zbw)):
        put = slice(which * n_chan, (which + 1) * n_chan)
        for b in range(2):
            rows_k = lax.broadcasted_iota(jnp.int32, (2 * SUB, n_chan), 0)
            w = [jnp.zeros((2 * SUB, n_chan), F32) for _ in range(2)]
            for k in range(n_lat):
                pair = ref[b, k].astype(F32)
                w = [jnp.where(rows_k == k, jnp.broadcast_to(pair[s:s + 1, :], rows_k.shape), w[s]) for s in range(2)]
            for s in range(2):
                zw[2 * b + s, 0:2 * SUB, put] = w[s].astype(BF16)
    zw[:, 2 * SUB:, :] = jnp.zeros((4, LANES - 2 * SUB, 2 * n_chan), BF16)

    def one_conv(conv, carry):
        slot = lax.rem(conv, 2)
        halo_wait(slot)

        @pl.when(conv == 0)
        def _():
            for q in range(4 * n_frame):
                zf[n_own + q * SUB:n_own + (q + 1) * SUB, :] = side_in[slot, q // n_frame, q % n_frame, :, zlane:wide].astype(F32)
            for q in range(4):
                at = n_own + (4 * n_frame + q) * SUB
                zf[at:at + SUB, :] = corner_in[slot, q, :, zlane:wide].astype(F32)

        latent_maps(conv)
        mean, inv = stats_finish(slot)
        scale = inv * par[conv, 0:1, :]
        offset = par[conv, 1:2, :]

        def act(v, at):
            normed = (v - mean) * scale + offset
            mixed = normed * zy[pl.ds(at, SUB), :] + zb[pl.ds(at, SUB), :]
            return rounded(mixed / (1.0 + jnp.exp(-mixed)))

        build(slot, act)

        def taps(step, carry):
            for i in range(GROUP):
                wait_chunk(lax.rem(conv * n_tap + step * GROUP + i, SLOTS))
            for kt in (2, 1, 0):
                lhs, rhs = [], []
                for i in range(GROUP):
                    p = step * GROUP + i
                    kh = p // 3
                    kw = p - 3 * kh
                    at = pl.multiple_of(kh * SUB, SUB)
                    lhs.append(xs[kw, 0:kt + 1, pl.ds(at, n_pos), :].reshape((kt + 1) * n_pos, n_chan).astype(BF16))
                    rhs.append(ring[lax.rem(conv * n_tap + p, SLOTS), kt])
                accs[kt][...] += dot_nt(jnp.concatenate(lhs, axis=1), jnp.concatenate(rhs, axis=1))
            for i in range(GROUP):
                refill(conv * n_tap + step * GROUP + i)
            return carry

        for ref in accs:
            ref[...] = jnp.zeros_like(ref)
        lax.fori_loop(0, n_tap // GROUP, taps, 0)

        odd = lax.rem(conv, 2) == 1
        s1 = jnp.zeros((SUB, n_chan), F32)
        s2 = jnp.zeros((SUB, n_chan), F32)
        bias = par[conv, 4:5, :]
        for at in range(0, n_pos, SUB):
            shared = acc_0[at:at + SUB, :] + bias
            for t in range(n_frame):
                early = max(t - 1, 0) * n_pos + at
                row = t * n_pos + at
                y = rounded(acc_2[row:row + SUB, :] + acc_1[early:early + SUB, :] + shared)
                old = xf[row:row + SUB, :]
                x = jnp.where(odd, rounded(old + y), y)
                xf[row:row + SUB, :] = jnp.where(odd, x, old)
                rf[row:row + SUB, :] = x
                s1 += x
                s2 += jnp.square(x)
        after = 1 - slot
        group_sums(after, jnp.concatenate([s1, s2], axis=0))

        @pl.when(conv < n_conv - 1)
        def _():
            stats_send(after)

        stage(rf, 0, n_chan)
        halo_start(after)
        return carry

    lax.fori_loop(0, n_conv, one_conv, 0)

    last = n_conv % 2
    halo_wait(last)
    build(last, lambda v, at: v)
    n_up = (n_row + 1) * n_col
    m_up = n_frame * n_up

    def up_row(kh, carry):
        ring_slot = lax.rem(n_conv * n_tap + kh, SLOTS)
        wait_chunk(ring_slot)
        at = pl.multiple_of(jnp.minimum(kh, 1) * SUB, SUB)
        x = [xs[d, :, pl.ds(at, n_up), :].reshape(m_up, n_chan).astype(BF16) for d in range(3)]
        for n in range(n_chan // TILE):
            cols = slice(n * TILE, (n + 1) * TILE)
            side_a = dot_nt(jnp.concatenate([x[0], x[1]], axis=0), ring[ring_slot, 0, cols, :])
            both = dot_nt(x[1], ring[ring_slot, 1, cols, :])
            side_b = dot_nt(jnp.concatenate([x[1], x[2]], axis=0), ring[ring_slot, 2, cols, :])
            tsum[kh, 0, :, cols] = side_a[0:m_up] + both + side_b[0:m_up]
            tsum[kh, 1, :, cols] = side_a[m_up:] + both + side_b[m_up:]
        return carry

    lax.fori_loop(0, 3, up_row, 0)
    bias_up = upb[...]

    def finish(g, carry):
        t = g // n_row
        i = g - t * n_row
        here = t * n_up + i * SUB
        for a in range(2):
            for b in range(2):
                v = bias_up
                for kh in range(3):
                    down = SUB if (a == 1 and kh != 1) else 0
                    v = v + tsum[kh, b, pl.ds(pl.multiple_of(here + down, SUB), SUB), :]
                for j in range(n_chan // LANES):
                    yout[a, j, pl.ds(b, SUB, stride=2), :] = v[:, j * LANES:(j + 1) * LANES]
            for j in range(n_chan // LANES):
                out[t, 2 * i + a, :, j * LANES:(j + 1) * LANES] = yout[a, j].astype(BF16)
        return carry

    lax.fori_loop(0, n_frame * n_row, finish, 0)


def solution(mesh):
    n_sh = mesh.shape["sh"]
    n_sw = mesh.shape["sw"]
    n_dev = n_sh * n_sw

    def local_step(features, latent, gn_gain, gn_bias, zy_weight, zy_bias, zb_weight, zb_bias, conv_weight, conv_bias, up_weight, up_bias):
        _, n_chan, n_frame, n_row, n_col = features.shape
        n_lat = latent.shape[1]
        n_pos = n_row * n_col
        n_own = n_frame * n_pos
        n_halo = (4 * n_frame + 4) * SUB
        feat = jnp.transpose(features, (0, 2, 3, 4, 1)).reshape(n_own, n_chan)
        lat = jnp.transpose(latent, (0, 2, 3, 4, 1)).reshape(n_own, n_lat)
        wconv = jnp.transpose(conv_weight, (0, 1, 4, 5, 6, 2, 3)).reshape(4, 3, 9, n_chan, n_chan)
        wup = jnp.transpose(up_weight, (2, 3, 0, 1)).reshape(9, n_chan, n_chan)
        zyw = jnp.transpose(zy_weight, (0, 2, 1, 3))
        zbw = jnp.transpose(zb_weight, (0, 2, 1, 3))
        vmem = pl.BlockSpec(memory_space=pltpu.VMEM)
        hbm = pl.BlockSpec(memory_space=pl.ANY)
        wide = n_chan + LANES
        y = pl.pallas_call(
            functools.partial(kernel, n_sh, n_sw, (n_chan, n_frame, n_row, n_col, n_lat)),
            out_shape=jax.ShapeDtypeStruct((n_frame, 2 * n_row, 2 * n_col, n_chan), BF16),
            in_specs=[vmem] * 10 + [hbm] * 2,
            out_specs=vmem,
            scratch_shapes=[
                pltpu.VMEM((SLOTS, 3, n_chan, n_chan), BF16),
                pltpu.VMEM((3, n_frame, (n_row + 2) * SUB, n_chan), F32),
                pltpu.VMEM((n_own, n_chan), F32),
                pltpu.VMEM((n_own, n_chan), F32),
                pltpu.VMEM((n_halo, n_chan), F32),
                pltpu.VMEM((n_own + n_halo, n_chan), F32),
                pltpu.VMEM((n_own + n_halo, n_chan), F32),
                pltpu.VMEM((n_own + n_halo, LANES), F32),
                pltpu.VMEM((4, LANES, 2 * n_chan), BF16),
                pltpu.VMEM((4, SUB, n_chan), F32),
                pltpu.VMEM((n_chan, LANES), BF16),
                pltpu.VMEM((LANES, n_chan), BF16),
                pltpu.VMEM((2 * SUB, n_chan), F32),
                pltpu.VMEM((2, LANES), F32),
                pltpu.VMEM((2, n_dev, 2, LANES), F32),
                pltpu.VMEM((4, n_frame, SUB, wide), BF16),
                pltpu.VMEM((4, SUB, wide), BF16),
                pltpu.VMEM((2, 4, n_frame, SUB, wide), BF16),
                pltpu.VMEM((2, 4, SUB, wide), BF16),
                pltpu.VMEM((n_pos, n_chan), F32),
                pltpu.VMEM((2 * n_pos, n_chan), F32),
                pltpu.VMEM((n_own, n_chan), F32),
                pltpu.VMEM((3, 2, n_frame * (n_row + 1) * n_col, n_chan), F32),
                pltpu.VMEM((2, n_chan // LANES, 2 * n_col, LANES), F32),
                pltpu.SemaphoreType.DMA((SLOTS,)),
                pltpu.SemaphoreType.DMA,
                pltpu.SemaphoreType.DMA((2,)),
                pltpu.SemaphoreType.DMA((8,)),
                pltpu.SemaphoreType.DMA((2, 8)),
            ],
            compiler_params=pltpu.CompilerParams(collective_id=0, has_side_effects=True, vmem_limit_bytes=VMEM_BYTES),
        )(feat, lat, gn_gain, gn_bias, zy_bias, zb_bias, conv_bias, zyw, zbw, up_bias.reshape(1, n_chan), wconv, wup)
        return jnp.transpose(y.reshape(1, n_frame, 2 * n_row, 2 * n_col, n_chan), (0, 4, 1, 2, 3))

    data_spec = P("dp", None, None, "sh", "sw")
    return jax.shard_map(local_step, mesh=mesh, in_specs=(data_spec, data_spec) + (P(),) * 10, out_specs=data_spec, check_vma=False)
```

time: 99.9 us -> 90.4 us (0.905)
  Pallas kernels: 96.1 us -> 86.6 us
    pallas_call x1, Pallas kernels: 96.1 us -> 86.6 us  [local_step(): pl.pallas_call(functools.partial(kernel, n_sh, n_sw, (n_chan, n_frame, n_...]
where the time goes in v2:
time: 90.4 us; the launch traced here: 90.3 us
  Pallas kernels  86.6 us (96%)
  local copies, waits for them, and re-layouts  3.63 us (4%)
    pallas_call x1, Pallas kernels, local_step(): pl.pallas_call(functools.partial(kernel, n_sh, n_sw, (n_chan, n_frame, n_...  86.6 us
    unnamed x1, local copies, waits for them, and re-layouts  2.37 us

profile of v2, /device:TPU:97, one launch (start us, length us, event | category | flops | bytes accessed | tf_op | source)
XLA Modules:
  0.0 90.3 jit_solution(6782904982154240355)
XLA Ops:
  0.0 1.3 %reshape.20.upb = f32[1,768]{1,0:T(1,128)} reshape(f32[768]{0:T(1024)} %param.23) | data formatting | bytes 6144 | tf_op jit(solution)/shard_map/reshape | solution.py:442
  1.3 86.6 %shard_map.118 = bf16[3,16,16,768]{3,2,1,0:T(8,128)(2,1)} custom-call(bf16[192,768]{1,0:T(8,128)(2,1)} %bitcast.19, bf16[192,12]{1,0:T(8,128)(2,1)} %bitcast.22, f32[2,2,768]{2,1,0:T(2,128)} %gain.1, f32[2,2,768]{2,1,0:T(2,128)} %shift.1, f32[2,2,768]{2,1,0:T(2,128)} %zyb.1, f32[2,2,768]{2,1,0:T(2,128)} %zbb.1, f32[2,2,768]{2,1,0:T(2,128)} %cb.1, ...), custom_call_target="tpu_custom_call" | custom-call | tf_op jit(solution)/shard_map/pallas_call | solution.py:405
  87.9 2.4 %copy.14 = bf16[1,768,3,16,16]{1,4,3,2,0:T(8,128)(2,1)} copy(bf16[1,768,3,16,16]{1,4,3,2,0:T(8,128)(2,1)} %bitcast.18) | data formatting | bytes 2359296

commit v3 on v2

--- a/solution.py
+++ b/solution.py
@@ -279,6 +279,8 @@
                 zf[at:at + SUB, :] = corner_in[slot, q, :, zlane:wide].astype(F32)
 
         latent_maps(conv)
+        for ref in accs:
+            ref[...] = jnp.zeros_like(ref)
         mean, inv = stats_finish(slot)
         scale = inv * par[conv, 0:1, :]
         offset = par[conv, 1:2, :]
@@ -303,12 +305,12 @@
                     lhs.append(xs[kw, 0:kt + 1, pl.ds(at, n_pos), :].reshape((kt + 1) * n_pos, n_chan).astype(BF16))
                     rhs.append(ring[lax.rem(conv * n_tap + p, SLOTS), kt])
                 accs[kt][...] += dot_nt(jnp.concatenate(lhs, axis=1), jnp.concatenate(rhs, axis=1))
-            for i in range(GROUP):
-                refill(conv * n_tap + step * GROUP + i)
+            @pl.when(step < n_tap // GROUP - 1)
+            def _():
+                for i in range(GROUP):
+                    refill(conv * n_tap + step * GROUP + i)
             return carry
 
-        for ref in accs:
-            ref[...] = jnp.zeros_like(ref)
         lax.fori_loop(0, n_tap // GROUP, taps, 0)
 
         odd = lax.rem(conv, 2) == 1
@@ -336,6 +338,8 @@
 
         stage(rf, 0, n_chan)
         halo_start(after)
+        for i in range(n_tap - GROUP, n_tap):
+            refill(conv * n_tap + i)
         return carry
 
     lax.fori_loop(0, n_conv, one_conv, 0)

time: 90.4 us -> 90.6 us (level)
  no operation moved by 1% of the time
where the time goes in v3:
time: 90.6 us; the launch traced here: 90.5 us
  Pallas kernels  86.8 us (96%)
  local copies, waits for them, and re-layouts  3.63 us (4%)
    pallas_call x1, Pallas kernels, local_step(): pl.pallas_call(functools.partial(kernel, n_sh, n_sw, (n_chan, n_frame, n_...  86.8 us
    unnamed x1, local copies, waits for them, and re-layouts  2.37 us

profile of v3, /device:TPU:97, one launch (start us, length us, event | category | flops | bytes accessed | tf_op | source)
XLA Modules:
  0.0 90.5 jit_solution(9741371457739739774)
XLA Ops:
  0.0 1.3 %reshape.20.upb = f32[1,768]{1,0:T(1,128)} reshape(f32[768]{0:T(1024)} %param.23) | data formatting | bytes 6144 | tf_op jit(solution)/shard_map/reshape | solution.py:446
  1.3 86.8 %shard_map.118 = bf16[3,16,16,768]{3,2,1,0:T(8,128)(2,1)} custom-call(bf16[192,768]{1,0:T(8,128)(2,1)} %bitcast.19, bf16[192,12]{1,0:T(8,128)(2,1)} %bitcast.22, f32[2,2,768]{2,1,0:T(2,128)} %gain.1, f32[2,2,768]{2,1,0:T(2,128)} %shift.1, f32[2,2,768]{2,1,0:T(2,128)} %zyb.1, f32[2,2,768]{2,1,0:T(2,128)} %zbb.1, f32[2,2,768]{2,1,0:T(2,128)} %cb.1, ...), custom_call_target="tpu_custom_call" | custom-call | tf_op jit(solution)/shard_map/pallas_call | solution.py:409
  88.1 2.4 %copy.14 = bf16[1,768,3,16,16]{1,4,3,2,0:T(8,128)(2,1)} copy(bf16[1,768,3,16,16]{1,4,3,2,0:T(8,128)(2,1)} %bitcast.18) | data formatting | bytes 2359296
